TPU v7x, 32 devices: a 4x4x1 block of a 4x4x8 slice. The times are simulated.
32 devices in a mesh: data: 1 (over z), pp: 4 (over y), ep: 8 (over x, core).
Axes of the slice: x: 4, y: 4, z: 1, core: 2. Of those that a mesh axis runs over, the one named last changes fastest.
The devices are a block of a 4x4x8 slice.
Arguments:
- expert_out: bfloat16 [4, 32, 2880, 1024], P(('data', 'pp'), 'ep')
- expert_ids: int32 [4, 24, 384, 8], P(('data', 'pp'), 'ep')
- slot_ids: int32 [4, 24, 384, 8], P(('data', 'pp'), 'ep')
- gate_vals: float32 [4, 24, 384, 8], P(('data', 'pp'), 'ep')
- residual: bfloat16 [4, 24, 384, 1024], P(('data', 'pp'), 'ep')
- norm_scale: float32 [4, 1024], P('pp')
- w_query: bfloat16 [4, 1024, 16, 64], P('pp')
- w_key: bfloat16 [4, 1024, 16, 64], P('pp')
- w_value: bfloat16 [4, 1024, 16, 64], P('pp')
- w_out: bfloat16 [4, 16, 64, 1024], P('pp')
Outputs:
- output: bfloat16 [4, 24, 384, 1024], P(('data', 'pp'), 'ep')
All inputs are finite; a program needn't handle non-finite values.
Results may differ from a plain program's by a relative error of at most 0.02.
Values are sent between devices in bfloat16 or wider.
A program may use at most 768 MiB of HBM per device.

v0:
```python
import jax
import jax.numpy as jnp
from jax import lax
from jax.sharding import PartitionSpec as P

NORM_EPS = 1e-6


def attn_block(merged, scale_vec, w_query, w_key, w_value, w_out):
    head_dim = w_query.shape[-1]
    seq_len = merged.shape[1]
    resid_f32 = merged.astype(jnp.float32)
    inv_rms = lax.rsqrt(jnp.mean(resid_f32 * resid_f32, axis=-1, keepdims=True) + NORM_EPS)
    normed_in = (resid_f32 * inv_rms * scale_vec).astype(jnp.bfloat16)
    q_heads = jnp.einsum('bld,dhe->blhe', normed_in, w_query, preferred_element_type=jnp.float32).astype(jnp.bfloat16)
    k_heads = jnp.einsum('bld,dhe->blhe', normed_in, w_key, preferred_element_type=jnp.float32).astype(jnp.bfloat16)
    v_heads = jnp.einsum('bld,dhe->blhe', normed_in, w_value, preferred_element_type=jnp.float32).astype(jnp.bfloat16)
    scores = jnp.einsum('bqhe,bkhe->bhqk', q_heads, k_heads, preferred_element_type=jnp.float32) * (head_dim ** -0.5)
    causal = jnp.arange(seq_len)[:, None] >= jnp.arange(seq_len)[None, :]
    scores = jnp.where(causal, scores, -1e30)
    exp_scores = jnp.exp(scores - jnp.max(scores, axis=-1, keepdims=True))
    row_sums = jnp.sum(exp_scores, axis=-1)
    mixed_vals = jnp.einsum('bhqk,bkhe->bqhe', exp_scores.astype(jnp.bfloat16), v_heads, preferred_element_type=jnp.float32)
    attn_out = (mixed_vals / jnp.swapaxes(row_sums, -1, -2)[..., None]).astype(jnp.bfloat16)
    proj_out = jnp.einsum('crif,ife->cre', attn_out, w_out, preferred_element_type=jnp.float32).astype(jnp.bfloat16)
    return (resid_f32 + proj_out.astype(jnp.float32)).astype(jnp.bfloat16)


def solution(mesh):
    ep_size = mesh.shape['ep']
    pp_size = mesh.shape['pp']
    next_stage = [(source, (source + 1) % pp_size) for source in range(pp_size)]
    token_spec = P(('data', 'pp'), 'ep', None, None)
    weight_spec = P('pp', None, None, None)

    def body(expert_out, expert_ids, slot_ids, gate_vals, residual, norm_scale, w_query, w_key, w_value, w_out):
        local_experts, capacity, model_width = expert_out.shape[1:]
        cap_dev = capacity // ep_size
        send_buf = expert_out[0].reshape(local_experts, ep_size, cap_dev, model_width)
        received = lax.all_to_all(send_buf, 'ep', 1, 0, tiled=True).reshape(-1, model_width)
        kept_mask = slot_ids[0] >= 0
        local_slot = slot_ids[0] - lax.axis_index('ep') * cap_dev
        row_ids = jnp.where(kept_mask, expert_ids[0] * cap_dev + local_slot, 0)
        gate_used = jnp.where(kept_mask, gate_vals[0], 0.0)
        picked_rows = jnp.take(received, row_ids, axis=0)
        merged = (residual[0].astype(jnp.float32) + jnp.sum(picked_rows * gate_used[..., None], axis=-2)).astype(jnp.bfloat16)
        arrived = lax.ppermute(merged, 'pp', next_stage)
        result = attn_block(arrived, norm_scale[0], w_query[0], w_key[0], w_value[0], w_out[0])
        return result[None]

    return jax.shard_map(body, mesh=mesh, in_specs=(token_spec, token_spec, token_spec, token_spec, token_spec, P('pp', None), weight_spec, weight_spec, weight_spec, weight_spec), out_specs=token_spec, check_vma=False)
```

profile of v0, /device:TPU:98, one launch (start us, length us, event | category | flops | bytes accessed | tf_op | source)
XLA Modules:
  0.0 475.9 jit_solution(16201411493540586784)
XLA Ops:
  0.0 0.0 copy-start
  0.0 20.1 %copy.19 = bf16[4,8,360,1024]{3,2,0,1:T(8,128)(2,1)} copy(bf16[4,8,360,1024]{3,2,1,0:T(8,128)(2,1)} %bitcast.78) | data formatting | bytes 47185920 | tf_op jit(solution)/shard_map/reshape;squeeze | solution.py:39
  20.1 0.0 copy-start.4
  20.1 0.0 copy-start.5
  20.1 0.0 copy-start.6
  20.1 7.3 %all-to-all-start = ((bf16[4,8,360,1024]{3,2,0,1:T(8,128)(2,1)}), bf16[4,8,360,1024]{3,2,0,1:T(8,128)(2,1)}, u32[]{:S(2)}, u32[]{:S(2)}) async-start(bf16[4,8,360,1024]{3,2,0,1:T(8,128)(2,1)} %copy.19), calls=%async_computation | async-start | bytes 47185920 | tf_op jit(solution)/shard_map/all_to_all | solution.py:40
  27.4 0.0 copy-done.4
  27.4 0.0 copy-done.5
  27.5 0.2 copy.20
  27.7 0.3 reshape.101
  28.0 0.9 copy.18
  28.9 0.0 copy-done.6
  28.9 0.2 copy.21
  29.2 254.4 %all-to-all-done = bf16[4,8,360,1024]{3,2,0,1:T(8,128)(2,1)} async-done(((bf16[4,8,360,1024]{3,2,0,1:T(8,128)(2,1)}), bf16[4,8,360,1024]{3,2,0,1:T(8,128)(2,1)}, u32[]{:S(2)}, u32[]{:S(2)}) %all-to-all-start) | async-done | bytes 23592992 | tf_op jit(solution)/shard_map/all_to_all | solution.py:40
  283.6 56.4 %gather_fusion = bf16[9216,1024]{1,0:T(8,128)(2,1)} fusion(bf16[11520,1024]{1,0:T(8,128)(2,1)} %bitcast.5, s32[9216]{0:T(1024)S(1)} %broadcast_clamp_fusion), kind=kCustom, calls=%fused_computation | custom fusion | bytes 37785600 | tf_op jit(solution)/shard_map/jit(_take)/gather | solution.py:45
  340.0 0.0 copy-start.3
  340.0 20.9 %multiply_reduce_fusion = f32[3,384,1024]{2,1,0:T(8,128)} fusion(f32[3,384,8]{2,1,0:T(8,128)S(1)} %copy.21, bf16[3,384,8,1024]{3,2,1,0:T(8,128)(2,1)} %bitcast.77, pred[3,384,8]{2,1,0:T(8,128)(4,1)} %copy.18), kind=kLoop, calls=%fused_computation.1 | loop fusion | flops 36569088 | bytes 23639040 | tf_op jit(solution)/shard_map/reduce_sum | solution.py:46
  360.8 0.0 copy-done.3
  360.8 0.0 copy-start.8
  360.8 3.3 fusion.10
  364.2 1.8 collective-permute-start
  366.0 53.3 %collective-permute-done = bf16[3,384,1024]{2,1,0:T(8,128)(2,1)S(1)} collective-permute-done((bf16[3,384,1024]{2,1,0:T(8,128)(2,1)S(1)}, bf16[3,384,1024]{2,1,0:T(8,128)(2,1)S(1)}, u32[]{:S(2)}, u32[]{:S(2)}) %collective-permute-start) | collective-permute-done | bytes 2359328 | tf_op jit(solution)/shard_map/ppermute | solution.py:47
  419.4 0.0 copy-start.1
  419.4 1.4 copy-done.1
  420.8 0.5 fusion.6
  421.3 0.0 copy-done
  421.3 0.0 copy-done.8
  421.3 17.3 %fusion = (f32[3,16,384]{2,1,0:T(8,128)S(1)}, f32[3,16,384,384]{2,3,1,0:T(8,128)}) fusion(pred[384,384]{0,1:T(8,128)(4,1)S(1)} %iota_compare_fusion, bf16[1,1024,16,64]{1,3,2,0:T(8,128)(2,1)S(1)} %copy-done, bf16[3,384,1024]{2,1,0:T(8,128)(2,1)} %copy-done.1, f32[1024]{0:T(1024)S(1)} %bitcast.80, f32[3,384]{1,0:T(4,128)S(1)} %add_rsqrt_fusion, ...), kind=kOutput, calls=%fused_computation.4 | convolution fusion | flops 5770819584 | bytes 35095040 | tf_op jit(solution)/shard_map/bqhe,bkhe->bhqk/dot_general | solution.py:18
  438.6 0.0 copy-start.2
  438.6 0.0 copy-start.7
  438.6 13.4 %fusion.1 = f32[3,16,384]{2,1,0:T(8,128)S(1)} fusion(f32[3,16,384,384]{2,3,1,0:T(8,128)} %get-tuple-element.6, f32[3,16,384]{2,1,0:T(8,128)S(1)} %get-tuple-element.5, pred[384,384]{0,1:T(8,128)(4,1)S(1)} %iota_compare_fusion), kind=kLoop, calls=%fused_computation.5 | loop fusion | flops 28293120 | bytes 28606464 | tf_op jit(solution)/shard_map/reduce_sum | solution.py:22
  452.0 0.0 copy-done.2
  452.0 0.0 copy-done.7
  452.0 4.5 fusion.35
  456.5 19.4 %fusion.18 = bf16[1,3,384,1024]{3,2,1,0:T(8,128)(2,1)} fusion(bf16[3,384,1024]{2,1,0:T(8,128)(2,1)} %copy-done.1, bf16[1,16,64,1024]{3,2,1,0:T(8,128)(2,1)} %param.19, f32[3,16,384,384]{2,3,1,0:T(8,128)} %get-tuple-element.6, f32[3,16,384]{2,1,0:T(8,128)S(1)} %get-tuple-element.5, pred[384,384]{0,1:T(8,128)(4,1)S(1)} %iota_compare_fusion, ...), kind=kOutput, calls=%fused_computation.22 | convolution fusion | flops 3358457856 | bytes 37781504 | tf_op jit(solution)/shard_map/crif,ife->cre/dot_general | solution.py:25
  (6 shorter events, 0.1 us)
Async XLA Ops:
  0.0 421.3 %copy-start = (bf16[1,1024,16,64]{1,3,2,0:T(8,128)(2,1)S(1)}, bf16[1,1024,16,64]{1,3,2,0:T(8,128)(2,1)}, u32[]{:S(2)}) copy-start(bf16[1,1024,16,64]{1,3,2,0:T(8,128)(2,1)} %param.17) | copy-start | bytes 6291460
  20.1 7.3 %copy-start.4 = (s32[1,3,384,8]{2,3,1,0:T(8,128)S(1)}, s32[1,3,384,8]{2,3,1,0:T(8,128)}, u32[]{:S(2)}) copy-start(s32[1,3,384,8]{2,3,1,0:T(8,128)} %param.12) | copy-start | bytes 110596
  20.1 7.3 %copy-start.5 = (s32[1,3,384,8]{2,3,1,0:T(8,128)S(1)}, s32[1,3,384,8]{2,3,1,0:T(8,128)}, u32[]{:S(2)}) copy-start(s32[1,3,384,8]{2,3,1,0:T(8,128)} %param.11) | copy-start | bytes 110596
  20.1 8.8 %copy-start.6 = (f32[1,3,384,8]{2,3,1,0:T(8,128)S(1)}, f32[1,3,384,8]{2,3,1,0:T(8,128)}, u32[]{:S(2)}) copy-start(f32[1,3,384,8]{2,3,1,0:T(8,128)} %param.13) | copy-start | bytes 110596
  20.1 263.5 %all-to-all-start = ((bf16[4,8,360,1024]{3,2,0,1:T(8,128)(2,1)}), bf16[4,8,360,1024]{3,2,0,1:T(8,128)(2,1)}, u32[]{:S(2)}, u32[]{:S(2)}) async-start(bf16[4,8,360,1024]{3,2,0,1:T(8,128)(2,1)} %copy.19), calls=%async_computation | async-start | bytes 47185920 | tf_op jit(solution)/shard_map/all_to_all | solution.py:40
  340.0 20.9 %copy-start.3 = (bf16[1,3,384,1024]{3,2,1,0:T(8,128)(2,1)S(1)}, bf16[1,3,384,1024]{3,2,1,0:T(8,128)(2,1)}, u32[]{:S(2)}) copy-start(bf16[1,3,384,1024]{3,2,1,0:T(8,128)(2,1)} %param.14) | copy-start | bytes 7077892
  360.8 60.5 %copy-start.8 = (f32[1,1024]{1,0:T(1,128)S(1)}, f32[1,1024]{1,0:T(1,128)}, u32[]{:S(2)}) copy-start(f32[1,1024]{1,0:T(1,128)} %param.15) | copy-start | bytes 12292
  364.2 55.2 %collective-permute-start = (bf16[3,384,1024]{2,1,0:T(8,128)(2,1)S(1)}, bf16[3,384,1024]{2,1,0:T(8,128)(2,1)S(1)}, u32[]{:S(2)}, u32[]{:S(2)}) collective-permute-start(bf16[3,384,1024]{2,1,0:T(8,128)(2,1)S(1)} %fusion.10), channel_id=1, source_target_pairs={{0,8},{8,16},{16,24},{24,0},{1,9},{9,17},{17,25},{25,1},{2,10},{10... | collective-permute-start | bytes 7077896 | tf_op jit(solution)/shard_map/ppermute | solution.py:47
  419.4 1.4 copy-start.1
  438.6 13.4 %copy-start.2 = (bf16[3,384,1024]{2,1,0:T(8,128)(2,1)S(1)}, bf16[3,384,1024]{2,1,0:T(8,128)(2,1)}, u32[]{:S(2)}) copy-start(bf16[3,384,1024]{2,1,0:T(8,128)(2,1)} %copy-done.1) | copy-start | bytes 7077892
  438.6 13.4 %copy-start.7 = (bf16[1,1024,16,64]{1,3,2,0:T(8,128)(2,1)S(1)}, bf16[1,1024,16,64]{1,3,2,0:T(8,128)(2,1)}, u32[]{:S(2)}) copy-start(bf16[1,1024,16,64]{1,3,2,0:T(8,128)(2,1)} %param.18) | copy-start | bytes 6291460
where the time goes:
time: 477 us; the launch traced here: 476 us
  waiting for transfers between devices  308 us (65%)
  local copies, waits for them, and re-layouts  79.5 us (17%)
  matrix products  41.2 us (9%)
  other arithmetic  38.2 us (8%)
  starting transfers between devices  9.13 us (2%)
    all_to_all x1, waiting for transfers between devices, body(): lax.all_to_all(send_buf, 'ep', 1, 0, tiled=True).reshape(-1, model_width)  254 us
    gather x1, local copies, waits for them, and re-layouts, body(): picked_rows = jnp.take(received, row_ids, axis=0)  56.4 us
    ppermute x1, waiting for transfers between devices, body(): arrived = lax.ppermute(merged, 'pp', next_stage)  53.3 us
    reduce_sum x1, other arithmetic, body(): jnp.sum(picked_rows * gate_used[..., None], axis=-2)  20.9 us
    another operation x1, local copies, waits for them, and re-layouts, body(): expert_out[0].reshape(local_experts, ep_size, cap_dev, model_width)  20.1 us
    dot_general x1, matrix products, attn_block(): jnp.einsum('crif,ife->cre', attn_out, w_out, preferred_element_type=jnp.f...  19.4 us
    dot_general x1, matrix products, attn_block(): jnp.einsum('bqhe,bkhe->bhqk', q_heads, k_heads, preferred_element_type=jn...  17.3 us
    reduce_sum x1, other arithmetic, attn_block(): row_sums = jnp.sum(exp_scores, axis=-1)  13.4 us
  transfers between devices with their start and end apart: 2, of which 2 were waited for; matrix products, arithmetic and copies ran while one was open for 0% of the time, Pallas kernels for 0%

commit v1 on v0

v1 whole, which is shorter than its diff:
```python
import functools

import jax
import jax.numpy as jnp
from jax import lax
from jax.experimental import pallas as pl
from jax.experimental.pallas import tpu as pltpu
from jax.sharding import PartitionSpec as P

NORM_EPS = 1e-6
CORES = 2
F32 = jnp.float32
BF16 = jnp.bfloat16
MESH = pl.DeviceIdType.MESH
NT = (((1,), (1,)), ((), ()))
SUBS = 3


def combine_kernel(dims, table, rows_hbm, resid_hbm, out_hbm, meta, own_rows, sib_rows, part, hop_in, dir_in, last_in,
                   resid, y_buf, meta_s, meta_r, sib_s, sib_r, own_sem, res_sem, hop_s, hop_r, dir_s, dir_r, last_s, last_r,
                   y_s, y_r):
    chips, stages, seqs, seq_len, cap, local = dims
    half = seq_len // 2
    sub = half // SUBS
    ep = lax.axis_index('ep')
    stage = lax.axis_index('pp')
    chip, core = ep // CORES, ep % CORES

    def dev(delta):
        return {'ep': ((chip + delta) % chips) * CORES + core}

    sibling = {'ep': chip * CORES + 1 - core}
    up = {'pp': (stage + 1) % stages}
    down = {'pp': (stage + stages - 1) % stages}
    right, left = dev(1), dev(chips - 1)

    def rows_of(rel, which):
        owner = ((chip + rel) % chips) * CORES + which
        return rows_hbm.at[:, pl.ds(pl.multiple_of(owner * cap, 8), cap), :]

    def meta_copy(rel):
        return pltpu.make_async_remote_copy(src_ref=table.at[(chip + chips - rel) % chips], dst_ref=meta.at[rel], send_sem=meta_s.at[rel],
                                            recv_sem=meta_r.at[rel], device_id=dev(chips - rel), device_id_type=MESH)

    def sib_copy(rel):
        return pltpu.make_async_remote_copy(src_ref=rows_of(rel, 1 - core), dst_ref=sib_rows.at[rel], send_sem=sib_s.at[rel],
                                            recv_sem=sib_r.at[rel], device_id=sibling, device_id_type=MESH)

    def own_copy(rel, slot):
        return pltpu.make_async_copy(rows_of(rel, core), own_rows.at[slot], own_sem.at[slot])

    def ring_copy(src, dst, ssem, rsem, way):
        return pltpu.make_async_remote_copy(src_ref=src, dst_ref=dst, send_sem=ssem, recv_sem=rsem,
                                            device_id=right if way == 0 else left, device_id_type=MESH)

    def hop_copy(way, s):
        return ring_copy(part.at[2, s, way], hop_in.at[way, s], hop_s.at[way, s], hop_r.at[way, s], way)

    def dir_copy(way, s):
        rel = 1 if way == 0 else chips - 1
        return ring_copy(part.at[rel, s, 1 - way], dir_in.at[way, s], dir_s.at[way, s], dir_r.at[way, s], way)

    def last_copy(way, s, u):
        rel = 1 if way == 0 else chips - 1
        span = pl.ds(pl.multiple_of(u * sub, 8), sub)
        return ring_copy(part.at[rel, s, way, span], last_in.at[way, s, span], last_s.at[way, s, u], last_r.at[way, s, u], way)

    def y_copy(s, w, u):
        span = pl.ds(pl.multiple_of(w * half + u * sub, 8), sub)
        return pltpu.make_async_remote_copy(src_ref=y_buf.at[s, span], dst_ref=out_hbm.at[s, span], send_sem=y_s.at[s, w, u],
                                            recv_sem=y_r.at[s, w, u], device_id=up, device_id_type=MESH)

    def order(k):
        return (2 + 3 * k) % chips

    own_copy(2, 0).start()
    res_copy = pltpu.make_async_copy(resid_hbm, resid, res_sem)
    res_copy.start()

    barrier = pltpu.get_barrier_semaphore()
    peers = (sibling, right, left, dev(2), up, down)
    for peer in peers:
        pl.semaphore_signal(barrier, inc=1, device_id=peer, device_id_type=MESH)
    pl.semaphore_wait(barrier, len(peers))

    for rel in (2, 3, 1):
        meta_copy(rel).start()
    for k in range(chips):
        sib_copy(order(k)).start()

    slot_iota = lax.broadcasted_iota(jnp.int32, (seq_len, cap), 1).astype(F32)

    def combine_step(n, carry):
        k, s = n // seqs, n % seqs
        rel = order(k)
        slot = k % 2

        @pl.when(s == 0)
        def _():
            own_copy(rel, slot).wait()
            sib_copy(rel).wait_recv()

            @pl.when(k < chips - 1)
            def _():
                own_copy(order(k + 1), 1 - slot).start()

            @pl.when(rel != 0)
            def _():
                meta_copy(rel).wait_recv()

            @pl.when(rel == 0)
            def _():
                meta[0] = table[chip]

        slots = meta[rel, 0, s].T
        gates = meta[rel, 1, s].T
        for e in range(CORES * local):
            pick = jnp.where(slots[:, e:e + 1] == slot_iota, 1.0, 0.0).astype(BF16)
            rows = own_rows[slot, e] if e < local else sib_rows[rel, e - local]
            term = gates[:, e:e + 1] * jnp.dot(pick, rows, preferred_element_type=F32)
            for w in range(2):
                piece = term[w * half:(w + 1) * half]
                if e == 0:
                    part[rel, s, w] = piece
                else:
                    part[rel, s, w] += piece

        @pl.when(rel == 2)
        def _():
            hop_copy(0, s).start()
            hop_copy(1, s).start()

        @pl.when(rel == 1)
        def _():
            dir_copy(0, s).start()

        @pl.when(rel == chips - 1)
        def _():
            dir_copy(1, s).start()

        return carry

    lax.fori_loop(0, chips * seqs, combine_step, 0)
    res_copy.wait()

    def relay_step(s, carry):
        for way in range(2):
            rel = 1 if way == 0 else chips - 1
            hop_copy(way, s).wait_recv()
            part[rel, s, way] += hop_in[way, s]
            for u in range(SUBS):
                last_copy(way, s, u).start()
        return carry

    lax.fori_loop(0, seqs, relay_step, 0)

    def final_step(n, carry):
        s, u = n // SUBS, n % SUBS
        span = pl.ds(pl.multiple_of(u * sub, 8), sub)

        @pl.when(u == 0)
        def _():
            dir_copy(0, s).wait_recv()
            dir_copy(1, s).wait_recv()

        for w in range(2):
            last_copy(w, s, u).wait_recv()
            whole = pl.ds(pl.multiple_of(w * half + u * sub, 8), sub)
            total = resid[s, whole].astype(F32) + part[0, s, w, span] + dir_in[1 - w, s, span] + last_in[w, s, span]
            y_buf[s, whole] = total.astype(BF16)
            y_copy(s, w, u).start()
        return carry

    lax.fori_loop(0, seqs * SUBS, final_step, 0)

    def drain(s, carry):
        for way in range(2):
            hop_copy(way, s).wait_send()
            dir_copy(way, s).wait_send()
            for u in range(SUBS):
                last_copy(way, s, u).wait_send()
                y_copy(s, way, u).wait()
        return carry

    for rel in (2, 3, 1):
        meta_copy(rel).wait_send()
    for k in range(chips):
        sib_copy(order(k)).wait_send()
    lax.fori_loop(0, seqs, drain, 0)


def attn_kernel(head_dim, y_ref, scale_ref, wq_ref, wk_ref, wv_ref, wo_ref, z_ref, q_buf, k_buf, v_buf, a_buf):
    seq_len, width = y_ref.shape
    pair = 2 * head_dim
    block = 128
    resid = y_ref[...].astype(F32)
    inv_rms = lax.rsqrt(jnp.mean(resid * resid, axis=-1, keepdims=True) + NORM_EPS)
    x = (resid * inv_rms * scale_ref[...]).astype(BF16)
    for w_ref, buf in ((wq_ref, q_buf), (wk_ref, k_buf), (wv_ref, v_buf)):
        buf[...] = lax.dot_general(x, w_ref[...], NT, preferred_element_type=F32).astype(BF16)
    low = lax.broadcasted_iota(jnp.int32, (block, pair), 1) < head_dim
    causal = lax.broadcasted_iota(jnp.int32, (block, block), 0) >= lax.broadcasted_iota(jnp.int32, (block, block), 1)

    def pair_step(p, carry):
        cols = pl.ds(pl.multiple_of(p * pair, pair), pair)
        for qb in range(seq_len // block):
            rows = slice(qb * block, (qb + 1) * block)
            keys = (qb + 1) * block
            q_pair = q_buf[rows, cols]
            k_pair = k_buf[0:keys, cols]
            v_pair = v_buf[0:keys, cols]
            outs = []
            for h in range(2):
                keep = low if h == 0 else jnp.logical_not(low)
                q_one = jnp.where(keep, q_pair.astype(F32), 0.0).astype(BF16)
                scores = lax.dot_general(q_one, k_pair, NT, preferred_element_type=F32) * (head_dim ** -0.5)
                diag = jnp.where(causal, scores[:, keys - block:], -1e30)
                scores = diag if qb == 0 else jnp.concatenate([scores[:, :keys - block], diag], axis=1)
                probs = jnp.exp(scores - jnp.max(scores, axis=-1, keepdims=True))
                sums = jnp.sum(probs, axis=-1, keepdims=True)
                outs.append(jnp.dot(probs.astype(BF16), v_pair, preferred_element_type=F32) / sums)
            a_buf[rows, cols] = jnp.where(low, outs[0], outs[1]).astype(BF16)
        return carry

    lax.fori_loop(0, width // pair, pair_step, 0)
    proj = jnp.dot(a_buf[...], wo_ref[...], preferred_element_type=F32).astype(BF16)
    z_ref[...] = (y_ref[...].astype(F32) + proj.astype(F32)).astype(BF16)


def solution(mesh):
    ep_size, pp_size = mesh.shape['ep'], mesh.shape['pp']
    chips = ep_size // CORES
    token_spec = P(('data', 'pp'), 'ep', None, None)
    weight_spec = P('pp', None, None, None)

    def body(expert_out, expert_ids, slot_ids, gate_vals, residual, norm_scale, w_query, w_key, w_value, w_out):
        local, capacity, width = expert_out.shape[1:]
        cap = capacity // ep_size
        seqs, seq_len = residual.shape[1:3]
        half, sub = seq_len // 2, seq_len // 2 // SUBS
        heads, head_dim = w_query.shape[2:]
        ep = lax.axis_index('ep')
        ids, slots, gates = (jnp.swapaxes(a[0], 1, 2)[None] for a in (expert_ids, slot_ids, gate_vals))
        number = jnp.arange(chips * CORES * local)
        core_flip = (number // local % CORES + ep % CORES) % CORES
        expert = (number // (CORES * local) * CORES + core_flip) * local + number % local
        match = (ids == expert[:, None, None, None]) & (slots >= 0)
        slot_of = jnp.max(jnp.where(match, slots - ep * cap, -1), axis=2).astype(F32)
        gate_of = jnp.sum(jnp.where(match, gates, 0.0), axis=2)
        table = jnp.stack([slot_of, gate_of]).reshape(2, chips, CORES * local, seqs, seq_len).transpose(1, 0, 3, 2, 4)

        dims = (chips, pp_size, seqs, seq_len, cap, local)
        dma = pltpu.SemaphoreType.DMA
        any_spec = pl.BlockSpec(memory_space=pl.ANY)
        vmem_spec = pl.BlockSpec(memory_space=pltpu.VMEM)
        arrived = pl.pallas_call(
            functools.partial(combine_kernel, dims),
            out_shape=jax.ShapeDtypeStruct((seqs, seq_len, width), BF16),
            in_specs=[vmem_spec, any_spec, any_spec],
            out_specs=any_spec,
            scratch_shapes=[
                pltpu.VMEM((chips, 2, seqs, CORES * local, seq_len), F32),
                pltpu.VMEM((2, local, cap, width), BF16),
                pltpu.VMEM((chips, local, cap, width), BF16),
                pltpu.VMEM((chips, seqs, 2, half, width), F32),
                pltpu.VMEM((2, seqs, half, width), F32),
                pltpu.VMEM((2, seqs, half, width), F32),
                pltpu.VMEM((2, seqs, half, width), F32),
                pltpu.VMEM((seqs, seq_len, width), BF16),
                pltpu.VMEM((seqs, seq_len, width), BF16),
                dma((chips,)), dma((chips,)), dma((chips,)), dma((chips,)), dma((2,)), dma,
                dma((2, seqs)), dma((2, seqs)), dma((2, seqs)), dma((2, seqs)),
                dma((2, seqs, SUBS)), dma((2, seqs, SUBS)), dma((seqs, 2, SUBS)), dma((seqs, 2, SUBS)),
            ],
            compiler_params=pltpu.CompilerParams(collective_id=0, has_side_effects=True, vmem_limit_bytes=67000000),
            name='combine',
        )(table, expert_out[0], residual[0])

        def flat_t(w):
            return jnp.transpose(w[0], (1, 2, 0)).reshape(heads * head_dim, width)

        full = pl.BlockSpec((heads * head_dim, width), lambda i: (0, 0))
        seq_block = pl.BlockSpec((None, seq_len, width), lambda i: (i, 0, 0))
        result = pl.pallas_call(
            functools.partial(attn_kernel, head_dim),
            grid=(seqs,),
            out_shape=jax.ShapeDtypeStruct((seqs, seq_len, width), BF16),
            in_specs=[seq_block, pl.BlockSpec((1, width), lambda i: (0, 0)), full, full, full, full],
            out_specs=seq_block,
            scratch_shapes=[pltpu.VMEM((seq_len, heads * head_dim), BF16)] * 4,
            compiler_params=pltpu.CompilerParams(vmem_limit_bytes=60000000),
            name='attention',
        )(arrived, norm_scale, flat_t(w_query), flat_t(w_key), flat_t(w_value), w_out[0].reshape(heads * head_dim, width))
        return result[None]

    return jax.shard_map(body, mesh=mesh, in_specs=(token_spec, token_spec, token_spec, token_spec, token_spec, P('pp', None), weight_spec, weight_spec, weight_spec, weight_spec), out_specs=token_spec, check_vma=False)
```

time: 477 us -> 239 us (0.50)
  waiting for transfers between devices: 308 us -> 0 us
  Pallas kernels: 0 us -> 233 us
  local copies, waits for them, and re-layouts: 79.5 us -> 0.01 us
  matrix products: 41.2 us -> 0 us
  other arithmetic: 38.2 us -> 5.21 us
  starting transfers between devices: 9.13 us -> 0 us
    all_to_all x1 -> x0, waiting for transfers between devices: 254 us -> none  [body(): lax.all_to_all(send_buf, 'ep', 1, 0, tiled=True).reshape(-1, model_width)]
    pallas_call x0 -> x2, Pallas kernels: none -> 233 us  [the longest x1 179 us: body(): pl.pallas_call(functools.partial(combine_kernel, dims), out_shape=jax.Sha...]
    gather x1 -> x0, local copies, waits for them, and re-layouts: 56.4 us -> none  [body(): picked_rows = jnp.take(received, row_ids, axis=0)]
    ppermute x1 -> x0, waiting for transfers between devices: 53.3 us -> none  [body(): arrived = lax.ppermute(merged, 'pp', next_stage)]
    dot_general x3 -> x0, matrix products: 41.2 us -> none  [the longest x1 19.4 us: attn_block(): jnp.einsum('crif,ife->cre', attn_out, w_out, preferred_element_type=jnp.f...]
    reduce_sum x3 -> x1, other arithmetic: 34.8 us -> 1.39 us  [body(): gate_of = jnp.sum(jnp.where(match, gates, 0.0), axis=2)]
    another operation x1, local copies, waits for them, and re-layouts: 20.1 us -> 0.01 us  [body(): jnp.stack([slot_of, gate_of])]
    all_to_all x1 -> x0, starting transfers between devices: 7.34 us -> none  [body(): lax.all_to_all(send_buf, 'ep', 1, 0, tiled=True).reshape(-1, model_width)]
  transfers between devices with their start and end apart: 2 -> 0, of which waited for: 2 -> 0; matrix products, arithmetic and copies ran while one was open for 0% -> 0% of each run, Pallas kernels for 0% -> 0%
where the time goes in v1:
time: 239 us
  Pallas kernels  233 us (97%)
  other arithmetic  5.21 us (2%)
    pallas_call x1, Pallas kernels, body(): pl.pallas_call(functools.partial(combine_kernel, dims), out_shape=jax.Sha...  179 us
    pallas_call x1, Pallas kernels, body(): pl.pallas_call(functools.partial(attn_kernel, head_dim), grid=(seqs,), ou...  54.5 us

profile of v1, /device:TPU:98, one launch (start us, length us, event | category | flops | bytes accessed | tf_op | source)
XLA Modules:
  0.0 238.6 jit_solution(6772784158671706913)
XLA Ops:
  0.0 0.8 compare_bitcast_fusion
  0.8 0.8 subtract_bitcast_fusion
  1.6 1.5 select_reduce_fusion.1
  3.1 1.4 select_reduce_fusion
  4.5 0.7 maximum_bitcast_fusion.table
  5.2 178.8 %combine.1.y_ref = bf16[3,384,1024]{2,1,0:T(8,128)(2,1)} custom-call(f32[4,2,3,8,384]{4,3,2,1,0:T(8,128)} %maximum_bitcast_fusion.table, bf16[4,2880,1024]{2,1,0:T(8,128)(2,1)} %bitcast.40, bf16[3,384,1024]{2,1,0:T(8,128)(2,1)} %bitcast.41), custom_call_target="tpu_custom_call" | custom-call | tf_op jit(solution)/shard_map/combine/pallas_call | solution.py:256
  184.1 54.5 %attention.1 = bf16[3,384,1024]{2,1,0:T(8,128)(2,1)} custom-call(bf16[3,384,1024]{2,1,0:T(8,128)(2,1)} %combine.1.y_ref, f32[1,1024]{1,0:T(1,128)} %scale_ref.1, bf16[1024,1024]{1,0:T(8,128)(2,1)} %bitcast.42, bf16[1024,1024]{1,0:T(8,128)(2,1)} %bitcast.43, bf16[1024,1024]{1,0:T(8,128)(2,1)} %bitcast.44, bf16[1024,1024]{1,0:T(8,128)(2,1)} %bitcast.45), custom_call_target="tpu_custom_call" | custom-call | tf_op jit(solution)/shard_map/attention/pallas_call | solution.py:284
  (2 shorter events, 0.0 us)

commit v2 on v1

v2 whole, which is shorter than its diff:
```python
import functools
import math

import jax
import jax.numpy as jnp
from jax import lax
from jax.experimental import pallas as pl
from jax.experimental.pallas import tpu as pltpu
from jax.sharding import PartitionSpec as P

NORM_EPS = 1e-6
CORES = 2
LAG = 2
BLOCK = 128
F32 = jnp.float32
BF16 = jnp.bfloat16
MESH = pl.DeviceIdType.MESH
NT = (((1,), (1,)), ((), ()))
TN = (((0,), (0,)), ((), ()))


def stage_kernel(dims, ids_hbm, slots_hbm, gates_hbm, rows_hbm, resid_hbm, scale, wq_hbm, wk_hbm, wv_hbm, wo_hbm, out_hbm,
                 ids_in, slots_in, gates_in, own_rows, sib_rows, part, hop_in, dir_in, last_in, resid, y_buf, y_in,
                 meta_s, meta_r, sib_s, sib_r, own_sem, res_sem, w_sem, hop_s, hop_r, dir_s, dir_r, last_s, last_r,
                 y_s, y_r, z_sem):
    chips, stages, seqs, seq_len, cap, local, head_dim = dims
    blocks = seq_len // BLOCK
    half, sub = seq_len // 2, BLOCK // 2
    width = own_rows.shape[-1]
    quarter = width // local
    heads_step = quarter // head_dim
    ep = lax.axis_index('ep')
    stage = lax.axis_index('pp')
    chip, core = ep // CORES, ep % CORES

    def dev(delta):
        return {'ep': ((chip + delta) % chips) * CORES + core}

    sibling = {'ep': chip * CORES + 1 - core}
    up = {'pp': (stage + 1) % stages}
    down = {'pp': (stage + stages - 1) % stages}
    right, left = dev(1), dev(chips - 1)

    def owner_of(rel, which):
        return ((chip + rel) % chips) * CORES + which

    def remote(src, dst, ssem, rsem, device):
        return pltpu.make_async_remote_copy(src_ref=src, dst_ref=dst, send_sem=ssem, recv_sem=rsem, device_id=device, device_id_type=MESH)

    meta_pairs = ((ids_hbm, ids_in), (slots_hbm, slots_in), (gates_hbm, gates_in))

    def meta_copy(rel, i):
        src, dst = meta_pairs[i]
        return remote(src, dst.at[rel], meta_s.at[i, rel], meta_r.at[i, rel], dev(chips - rel))

    def meta_local(i):
        src, dst = meta_pairs[i]
        return pltpu.make_async_copy(src, dst.at[0], meta_r.at[i, 0])

    def sib_copy(rel, e):
        rows = pl.ds(pl.multiple_of(owner_of(rel, 1 - core) * cap, 8), cap)
        return remote(rows_hbm.at[e, rows], sib_rows.at[rel, e], sib_s.at[rel, e], sib_r.at[rel, e], sibling)

    def own_copy(rel, slot):
        rows = pl.ds(pl.multiple_of(owner_of(rel, core) * cap, 8), cap)
        return pltpu.make_async_copy(rows_hbm.at[:, rows], own_rows.at[slot], own_sem.at[slot])

    def weight_copy(i, j):
        src = (wq_hbm, wk_hbm, wv_hbm, wo_hbm)[i]
        return pltpu.make_async_copy(src.at[j * quarter:(j + 1) * quarter], sib_rows.at[i, j, 0:quarter], w_sem.at[i, j])

    def ring_copy(src, dst, ssem, rsem, way):
        return remote(src, dst, ssem, rsem, right if way == 0 else left)

    def hop_copy(way, s):
        return ring_copy(part.at[2, s, way], hop_in.at[way, s], hop_s.at[way, s], hop_r.at[way, s], way)

    def dir_copy(way, s):
        rel = 1 if way == 0 else chips - 1
        return ring_copy(part.at[rel, s, 1 - way], dir_in.at[way, s], dir_s.at[way, s], dir_r.at[way, s], way)

    def last_copy(way, s, u):
        rel = 1 if way == 0 else chips - 1
        span = pl.ds(u * sub, sub)
        return ring_copy(part.at[rel, s, way, span], last_in.at[way, s, span], last_s.at[way, s, u], last_r.at[way, s, u], way)

    def y_copy(s, u):
        span = pl.ds(u * BLOCK, BLOCK)
        return remote(y_buf.at[s, span], y_in.at[s, span], y_s.at[s, u], y_r.at[s, u], up)

    def z_copy(s, u):
        span = pl.ds(u * BLOCK, BLOCK)
        return pltpu.make_async_copy(y_buf.at[s, span], out_hbm.at[s, span], z_sem.at[s, u])

    def order(k):
        return (2 + 3 * k) % chips

    own_copy(2, 0).start()
    own_copy(order(1), 1).start()
    for i in range(3):
        meta_local(i).start()
    res_copy = pltpu.make_async_copy(resid_hbm, resid, res_sem)
    res_copy.start()

    barrier = pltpu.get_barrier_semaphore()
    peers = (sibling, right, left, dev(2), up, down)
    for peer in peers:
        pl.semaphore_signal(barrier, inc=1, device_id=peer, device_id_type=MESH)
    pl.semaphore_wait(barrier, len(peers))

    for rel in (2, 3, 1):
        for i in range(3):
            meta_copy(rel, i).start()
    for k in range(chips):
        for e in range(local):
            sib_copy(order(k), e).start()

    slot_iota = lax.broadcasted_iota(jnp.int32, (seq_len, cap), 1).astype(F32)
    expert_iota = lax.broadcasted_iota(jnp.int32, (CORES * local, seq_len), 0)

    def combine_block(rel, s, slot, before):
        ids, slots, gates = ids_in[rel, s], slots_in[rel, s], gates_in[rel, s]
        kept = slots >= 0
        local_slot = (slots - owner_of(rel, core) * cap).astype(F32)
        slot_rows = jnp.full((CORES * local, seq_len), -1.0, F32)
        gate_rows = jnp.zeros((CORES * local, seq_len), F32)
        for e in range(CORES * local):
            expert = (chip * CORES + (core if e < local else 1 - core)) * local + e % local
            match = jnp.logical_and(ids == expert, kept)
            slot_e = jnp.max(jnp.where(match, local_slot, -1.0), axis=0, keepdims=True)
            gate_e = jnp.sum(jnp.where(match, gates, 0.0), axis=0, keepdims=True)
            slot_rows = jnp.where(expert_iota == e, slot_e, slot_rows)
            gate_rows = jnp.where(expert_iota == e, gate_e, gate_rows)
        slot_cols, gate_cols = slot_rows.T, gate_rows.T
        for e in range(CORES * local):
            before(e)
            pick = jnp.where(slot_cols[:, e:e + 1] == slot_iota, 1.0, 0.0).astype(BF16)
            rows = own_rows[slot, e] if e < local else sib_rows[rel, e - local]
            term = gate_cols[:, e:e + 1] * jnp.dot(pick, rows, preferred_element_type=F32)
            for u in range(blocks):
                for w in range(2):
                    piece = term[u * BLOCK + w * sub:u * BLOCK + (w + 1) * sub]
                    if e == 0:
                        part[rel, s, w, u * sub:(u + 1) * sub] = piece
                    else:
                        part[rel, s, w, u * sub:(u + 1) * sub] += piece

    def first_wait(e):
        if e >= local:
            sib_copy(2, e - local).wait_recv()

    for i in range(3):
        meta_copy(2, i).wait_recv()
    own_copy(2, 0).wait()
    combine_block(2, 0, 0, first_wait)
    hop_copy(0, 0).start()
    hop_copy(1, 0).start()

    def combine_step(n, carry):
        k, s = n // seqs, n % seqs
        rel = order(k)
        slot = k % 2

        @pl.when(s == 0)
        def _():
            own_copy(rel, slot).wait()
            for e in range(local):
                sib_copy(rel, e).wait_recv()

            @pl.when(k < chips - 1)
            def _():
                own_copy(order(k + 1), 1 - slot).start()

            @pl.when(rel != 0)
            def _():
                for i in range(3):
                    meta_copy(rel, i).wait_recv()

            @pl.when(rel == 0)
            def _():
                for i in range(3):
                    meta_local(i).wait()

        combine_block(rel, s, slot, lambda e: None)

        @pl.when(rel == 2)
        def _():
            hop_copy(0, s).start()
            hop_copy(1, s).start()

        @pl.when(rel == 1)
        def _():
            dir_copy(0, s).start()

        @pl.when(rel == chips - 1)
        def _():
            dir_copy(1, s).start()

        return carry

    lax.fori_loop(1, chips * seqs, combine_step, 0)
    for i in range(4):
        for j in range(local):
            weight_copy(i, j).start()
    res_copy.wait()

    def relay_step(s, carry):
        for way in range(2):
            rel = 1 if way == 0 else chips - 1
            hop_copy(way, s).wait_recv()
            part[rel, s, way] += hop_in[way, s]
            for u in range(blocks):
                last_copy(way, s, u).start()
        return carry

    lax.fori_loop(0, seqs, relay_step, 0)
    for i in range(4):
        for j in range(local):
            weight_copy(i, j).wait()

    def merge_block(s, u):
        if u == 0:
            dir_copy(0, s).wait_recv()
            dir_copy(1, s).wait_recv()
        span = slice(u * sub, (u + 1) * sub)
        for w in range(2):
            last_copy(w, s, u).wait_recv()
            whole = slice(u * BLOCK + w * sub, u * BLOCK + (w + 1) * sub)
            total = resid[s, whole].astype(F32) + part[0, s, w, span] + dir_in[1 - w, s, span] + last_in[w, s, span]
            y_buf[s, whole] = total.astype(BF16)
        y_copy(s, u).start()

    factor = head_dim ** -0.5 * math.log2(math.e)
    causal = lax.broadcasted_iota(jnp.int32, (BLOCK, BLOCK), 0) <= lax.broadcasted_iota(jnp.int32, (BLOCK, BLOCK), 1)
    a_cols = slice(seq_len, seq_len + BLOCK)
    q_cols = slice(2 * seq_len, 2 * seq_len + BLOCK)

    def attend_block(s, u):
        y_copy(s, u).wait_recv()
        keys = (u + 1) * BLOCK
        here = slice(u * BLOCK, (u + 1) * BLOCK)
        y = y_in[s, here].astype(F32)
        inv_rms = lax.rsqrt(jnp.mean(y * y, axis=-1, keepdims=True) + NORM_EPS)
        x = (y * inv_rms * scale[...]).astype(BF16)
        for i, (plane, cols) in enumerate(((0, q_cols), (0, here), (1, here))):
            for j in range(local):
                heads = lax.dot_general(sib_rows[i, j, 0:quarter], x, NT, preferred_element_type=F32)
                own_rows[plane, j, 0:quarter, cols] = heads.astype(BF16)

        def heads_of(j, carry):
            spans = [slice(h * head_dim, (h + 1) * head_dim) for h in range(heads_step)]
            scores = [lax.dot_general(own_rows[0, j, r, 0:keys], own_rows[0, j, r, q_cols], TN, preferred_element_type=F32) for r in spans]
            probs, sums = [], []
            for t in scores:
                diag = jnp.where(causal, t[keys - BLOCK:], -1e30)
                t = diag if u == 0 else jnp.concatenate([t[:keys - BLOCK], diag], axis=0)
                t = jnp.exp2((t - jnp.max(t, axis=0, keepdims=True)) * factor)
                sums.append(jnp.sum(t, axis=0, keepdims=True))
                probs.append(t.astype(BF16))
            for r, t, total in zip(spans, probs, sums):
                mixed = jnp.dot(own_rows[1, j, r, 0:keys], t, preferred_element_type=F32)
                own_rows[1, j, r, a_cols] = (mixed / total).astype(BF16)
            return carry

        lax.fori_loop(0, local, heads_of, 0)
        proj = lax.dot_general(own_rows[1, 0, 0:quarter, a_cols], sib_rows[3, 0, 0:quarter], TN, preferred_element_type=F32)
        for j in range(1, local):
            proj += lax.dot_general(own_rows[1, j, 0:quarter, a_cols], sib_rows[3, j, 0:quarter], TN, preferred_element_type=F32)
        z = y_in[s, here].astype(F32) + proj.astype(BF16).astype(F32)
        y_copy(s, u).wait_send()
        y_buf[s, here] = z.astype(BF16)
        z_copy(s, u).start()

    def final_step(s, carry):
        for u in range(blocks):
            back = u - LAG
            past, at = (s, back) if back >= 0 else (s - 1, back + blocks)

            @pl.when(s < seqs)
            def _():
                merge_block(s, u)
                if back >= 0:
                    attend_block(past, at)

            if back < 0:
                @pl.when(s > 0)
                def _():
                    attend_block(past, at)
        return carry

    lax.fori_loop(0, seqs + 1, final_step, 0)

    def drain(s, carry):
        for way in range(2):
            hop_copy(way, s).wait_send()
            dir_copy(way, s).wait_send()
            for u in range(blocks):
                last_copy(way, s, u).wait_send()
        for u in range(blocks):
            z_copy(s, u).wait()
        return carry

    for rel in (2, 3, 1):
        for i in range(3):
            meta_copy(rel, i).wait_send()
    for k in range(chips):
        for e in range(local):
            sib_copy(order(k), e).wait_send()
    lax.fori_loop(0, seqs, drain, 0)


def solution(mesh):
    ep_size, pp_size = mesh.shape['ep'], mesh.shape['pp']
    chips = ep_size // CORES
    token_spec = P(('data', 'pp'), 'ep', None, None)
    weight_spec = P('pp', None, None, None)

    def body(expert_out, expert_ids, slot_ids, gate_vals, residual, norm_scale, w_query, w_key, w_value, w_out):
        local, capacity, width = expert_out.shape[1:]
        cap = capacity // ep_size
        seqs, seq_len, tops = expert_ids.shape[1:]
        half, blocks = seq_len // 2, seq_len // BLOCK
        heads, head_dim = w_query.shape[2:]
        routing = [jnp.swapaxes(a[0], 1, 2) for a in (expert_ids, slot_ids, gate_vals)]

        def flat_t(w):
            return jnp.transpose(w[0], (1, 2, 0)).reshape(heads * head_dim, width)

        dims = (chips, pp_size, seqs, seq_len, cap, local, head_dim)
        dma = pltpu.SemaphoreType.DMA
        any_spec = pl.BlockSpec(memory_space=pl.ANY)
        vmem_spec = pl.BlockSpec(memory_space=pltpu.VMEM)
        result = pl.pallas_call(
            functools.partial(stage_kernel, dims),
            out_shape=jax.ShapeDtypeStruct((seqs, seq_len, width), BF16),
            in_specs=[any_spec] * 5 + [vmem_spec] + [any_spec] * 4,
            out_specs=any_spec,
            scratch_shapes=[
                pltpu.VMEM((chips, seqs, tops, seq_len), jnp.int32),
                pltpu.VMEM((chips, seqs, tops, seq_len), jnp.int32),
                pltpu.VMEM((chips, seqs, tops, seq_len), F32),
                pltpu.VMEM((2, local, cap, width), BF16),
                pltpu.VMEM((chips, local, cap, width), BF16),
                pltpu.VMEM((chips, seqs, 2, half, width), F32),
                pltpu.VMEM((2, seqs, half, width), F32),
                pltpu.VMEM((2, seqs, half, width), F32),
                pltpu.VMEM((2, seqs, half, width), F32),
                pltpu.VMEM((seqs, seq_len, width), BF16),
                pltpu.VMEM((seqs, seq_len, width), BF16),
                pltpu.VMEM((seqs, seq_len, width), BF16),
                dma((3, chips)), dma((3, chips)), dma((chips, local)), dma((chips, local)), dma((2,)), dma, dma((4, local)),
                dma((2, seqs)), dma((2, seqs)), dma((2, seqs)), dma((2, seqs)),
                dma((2, seqs, blocks)), dma((2, seqs, blocks)), dma((seqs, blocks)), dma((seqs, blocks)), dma((seqs, blocks)),
            ],
            compiler_params=pltpu.CompilerParams(collective_id=0, has_side_effects=True, vmem_limit_bytes=67000000),
            name='stage',
        )(*routing, expert_out[0], residual[0], norm_scale, flat_t(w_query), flat_t(w_key), flat_t(w_value),
          w_out[0].reshape(heads * head_dim, width))
        return result[None]

    return jax.shard_map(body, mesh=mesh, in_specs=(token_spec, token_spec, token_spec, token_spec, token_spec, P('pp', None), weight_spec, weight_spec, weight_spec, weight_spec), out_specs=token_spec, check_vma=False)
```

time: 239 us -> 189 us (0.79)
  Pallas kernels: 233 us -> 186 us
  other arithmetic: 5.21 us -> 0 us
  local copies, waits for them, and re-layouts: 0.01 us -> 3.27 us
    pallas_call x2 -> x1, Pallas kernels: 233 us -> 186 us  [body(): pl.pallas_call(functools.partial(stage_kernel, dims), out_shape=jax.Shape...]
    unnamed x0 -> x1, local copies, waits for them, and re-layouts: none -> 3.27 us
where the time goes in v2:
time: 189 us
  Pallas kernels  186 us (98%)
  local copies, waits for them, and re-layouts  3.27 us (2%)
    pallas_call x1, Pallas kernels, body(): pl.pallas_call(functools.partial(stage_kernel, dims), out_shape=jax.Shape...  186 us

profile of v2, /device:TPU:98, one launch (start us, length us, event | category | flops | bytes accessed | tf_op | source)
XLA Modules:
  0.0 188.8 jit_solution(12673956303405634571)
XLA Ops:
  0.0 185.6 %stage.1 = bf16[3,384,1024]{2,1,0:T(8,128)(2,1)} custom-call(s32[3,8,384]{2,1,0:T(8,128)} %bitcast.35, s32[3,8,384]{2,1,0:T(8,128)} %bitcast.36, f32[3,8,384]{2,1,0:T(8,128)} %bitcast.37, bf16[4,2880,1024]{2,1,0:T(8,128)(2,1)} %bitcast.28, bf16[3,384,1024]{2,1,0:T(8,128)(2,1)} %bitcast.30, f32[1,1024]{1,0:T(1,128)} %scale.1, bf16[1024,1024]{1,0:T(8,128)(2,1)} %bitcast.31, ...), custom_call_target="tpu_custom_call" | custom-call | tf_op jit(solution)/shard_map/stage/pallas_call | solution.py:333
  185.6 3.3 %copy.12 = bf16[1,3,384,1024]{3,2,1,0:T(8,128)(2,1)} copy(bf16[1,3,384,1024]{3,2,1,0:T(8,128)(2,1)} %bitcast.29) | data formatting | bytes 4718592

commit v3 on v2

v3 whole, which is shorter than its diff:
```python
import functools
import math

import jax
import jax.numpy as jnp
from jax import lax
from jax.experimental import pallas as pl
from jax.experimental.pallas import tpu as pltpu
from jax.sharding import PartitionSpec as P

NORM_EPS = 1e-6
NONE = -256.0
CORES = 2
BLOCK = 128
PIECES = (1, 2, 4)
STRIPS = 4
PAIRS = 4
F32 = jnp.float32
BF16 = jnp.bfloat16
MESH = pl.DeviceIdType.MESH
NT = (((1,), (1,)), ((), ()))
TN = (((0,), (0,)), ((), ()))


def stage_kernel(dims, ids_hbm, slots_hbm, gates_hbm, rows_hbm, resid_hbm, scale, wq_hbm, wk_hbm, wv_hbm, wo_hbm, out_ref,
                 ids_in, slots_in, gates_in, slot_out, gate_out, slot_in, gate_in, own_rows, sib_rows, part, hop_in, dir_in, last_in, resid, y_buf, y_in,
                 in_sem, meta_s, meta_r, sib_s, sib_r, own_sem, res_sem, w_sem, hop_s, hop_r, dir_s, dir_r, last_s, last_r,
                 y_s, y_r):
    chips, stages, seqs, seq_len, cap, local, head_dim = dims
    blocks = seq_len // BLOCK
    half, sub = seq_len // 2, BLOCK // 2
    strip = sub // STRIPS
    width = own_rows.shape[-1]
    quarter = width // local
    heads_step = quarter // head_dim
    ep = lax.axis_index('ep')
    stage = lax.axis_index('pp')
    chip, core = ep // CORES, ep % CORES

    def dev(delta):
        return {'ep': ((chip + delta) % chips) * CORES + core}

    sibling = {'ep': chip * CORES + 1 - core}
    up = {'pp': (stage + 1) % stages}
    down = {'pp': (stage + stages - 1) % stages}
    right, left = dev(1), dev(chips - 1)

    def owner_of(rel, which):
        return ((chip + rel) % chips) * CORES + which

    def remote(src, dst, ssem, rsem, device):
        return pltpu.make_async_remote_copy(src_ref=src, dst_ref=dst, send_sem=ssem, recv_sem=rsem, device_id=device, device_id_type=MESH)

    def in_copy(i):
        src, dst = ((ids_hbm, ids_in), (slots_hbm, slots_in), (gates_hbm, gates_in))[i]
        return pltpu.make_async_copy(src, dst, in_sem.at[i])

    def meta_copy(rel, s, i):
        src, dst = ((slot_out, slot_in), (gate_out, gate_in))[i]
        return remote(src.at[rel, s], dst.at[rel, s], meta_s.at[i, rel, s], meta_r.at[i, rel, s], dev(chips - rel))

    def sib_copy(rel, e):
        rows = pl.ds(pl.multiple_of(owner_of(rel, 1 - core) * cap, 8), cap)
        return remote(rows_hbm.at[e, rows], sib_rows.at[rel, e], sib_s.at[rel, e], sib_r.at[rel, e], sibling)

    def own_copy(rel, slot):
        rows = pl.ds(pl.multiple_of(owner_of(rel, core) * cap, 8), cap)
        return pltpu.make_async_copy(rows_hbm.at[:, rows], own_rows.at[slot], own_sem.at[slot])

    def weight_copy(i, j):
        src = (wq_hbm, wk_hbm, wv_hbm, wo_hbm)[i]
        return pltpu.make_async_copy(src.at[j * quarter:(j + 1) * quarter], sib_rows.at[i, j, 0:quarter], w_sem.at[i, j])

    def ring_copy(src, dst, ssem, rsem, way):
        return remote(src, dst, ssem, rsem, right if way == 0 else left)

    def hop_copy(way, s):
        return ring_copy(part.at[2, s, way], hop_in.at[way, s], hop_s.at[way, s], hop_r.at[way, s], way)

    def dir_copy(way, s, u):
        rel = 1 if way == 0 else chips - 1
        span = pl.ds(u * sub, sub)
        return ring_copy(part.at[rel, s, 1 - way, span], dir_in.at[way, s, span], dir_s.at[way, s, u], dir_r.at[way, s, u], way)

    def last_copy(way, s, u, p):
        rel = 1 if way == 0 else chips - 1
        rows, i = sub // PIECES[u], sum(PIECES[:u]) + p
        span = pl.ds(u * sub + p * rows, rows)
        return ring_copy(part.at[rel, s, way, span], last_in.at[way, s, span], last_s.at[way, s, i], last_r.at[way, s, i], way)

    def y_copy(s, u, p):
        rows, i = BLOCK // PIECES[u], sum(PIECES[:u]) + p
        span = pl.ds(u * BLOCK + p * rows, rows)
        return remote(y_buf.at[s, span], y_in.at[s, span], y_s.at[s, i], y_r.at[s, i], up)

    def order(k):
        return (2 + 3 * (k + k // 2 - 2 * (k // 3))) % chips

    for i in range(3):
        in_copy(i).start()
    own_copy(2, 0).start()
    own_copy(1, 1).start()
    res_copy = pltpu.make_async_copy(resid_hbm, resid, res_sem)
    res_copy.start()

    barrier = pltpu.get_barrier_semaphore()
    peers = (sibling, right, left, dev(2), up, down)
    for peer in peers:
        pl.semaphore_signal(barrier, inc=1, device_id=peer, device_id_type=MESH)

    for i in range(3):
        in_copy(i).wait()
    expert_iota = lax.broadcasted_iota(jnp.int32, (CORES * local, seq_len), 0)

    def table_step(s, carry):
        ids, gates = ids_in[s], gates_in[s]
        kept = slots_in[s] >= 0
        code = (slots_in[s] - (ep * cap + cap // 2)).astype(F32)
        for rel in (2, 1, 0, 3):
            target = (chip + chips - rel) % chips
            slot_rows = jnp.full((CORES * local, seq_len), NONE, F32)
            gate_rows = jnp.zeros((CORES * local, seq_len), F32)
            for e in range(CORES * local):
                expert = (target * CORES + (core if e < local else 1 - core)) * local + e % local
                match = jnp.logical_and(ids == expert, kept)
                slot_e = jnp.max(jnp.where(match, code, NONE), axis=0, keepdims=True)
                gate_e = jnp.sum(jnp.where(match, gates, 0.0), axis=0, keepdims=True)
                slot_rows = jnp.where(expert_iota == e, slot_e, slot_rows)
                gate_rows = jnp.where(expert_iota == e, gate_e, gate_rows)
            slot_to, gate_to = (slot_in, gate_in) if rel == 0 else (slot_out, gate_out)
            slot_to[rel, s] = slot_rows.astype(BF16)
            gate_to[rel, s] = gate_rows
        return carry

    lax.fori_loop(0, seqs, table_step, 0)
    pl.semaphore_wait(barrier, len(peers))

    for s in range(seqs):
        for rel in (2, 1, 3):
            for i in range(2):
                meta_copy(rel, s, i).start()
    for k in range(chips):
        for e in range(local):
            sib_copy(order(k), e).start()

    slot_iota = (lax.broadcasted_iota(jnp.int32, (seq_len, cap), 1) - cap // 2).astype(F32)

    def combine_block(rel, s, slot, before):
        slot_cols, gate_cols = slot_in[rel, s].astype(F32).T, gate_in[rel, s].T
        for e in range(CORES * local):
            before(e)
            pick = jnp.where(slot_cols[:, e:e + 1] == slot_iota, 1.0, 0.0).astype(BF16)
            rows = own_rows[slot, e] if e < local else sib_rows[rel, e - local]
            term = gate_cols[:, e:e + 1] * jnp.dot(pick, rows, preferred_element_type=F32)
            for i in range(half // strip):
                for w in range(2):
                    piece = term[(2 * i + w) * strip:(2 * i + w + 1) * strip]
                    if e == 0:
                        part[rel, s, w, i * strip:(i + 1) * strip] = piece
                    else:
                        part[rel, s, w, i * strip:(i + 1) * strip] += piece

    def first_wait(e):
        if e >= local:
            sib_copy(2, e - local).wait_recv()

    own_copy(2, 0).wait()
    for i in range(2):
        meta_copy(2, 0, i).wait_recv()
    combine_block(2, 0, 0, first_wait)
    hop_copy(0, 0).start()
    hop_copy(1, 0).start()

    def relay(s, last):
        for way in range(2):
            rel = 1 if way == 0 else chips - 1
            hop_copy(way, s).wait_recv()
            part[rel, s, way] += hop_in[way, s]
        for u in range(blocks):
            for way in range(2):
                if last:
                    dir_copy(way, s, u).start()
                for p in range(PIECES[u]):
                    last_copy(way, s, u, p).start()

    def combine_step(n, carry):
        s, k = n // chips, n % chips
        rel = order(k)
        slot = n % 2

        @pl.when(n < seqs * chips - 1)
        def _():
            own_copy(order((n + 1) % chips), 1 - slot).start()

        @pl.when(n == chips + 1)
        def _():
            relay(0, False)

        own_copy(rel, slot).wait()

        @pl.when(s == 0)
        def _():
            for e in range(local):
                sib_copy(rel, e).wait_recv()

        @pl.when(rel != 0)
        def _():
            for i in range(2):
                meta_copy(rel, s, i).wait_recv()

        combine_block(rel, s, slot, lambda e: None)

        @pl.when(rel == 2)
        def _():
            hop_copy(0, s).start()
            hop_copy(1, s).start()

        for way, ready in ((0, 1), (1, chips - 1)):
            @pl.when(jnp.logical_and(rel == ready, s < seqs - 1))
            def _():
                for u in range(blocks):
                    dir_copy(way, s, u).start()

        return carry

    lax.fori_loop(1, chips * seqs, combine_step, 0)
    for i in range(4):
        for j in range(local):
            weight_copy(i, j).start()
    res_copy.wait()
    relay(1, False)
    for i in range(4):
        for j in range(local):
            weight_copy(i, j).wait()

    def merge_block(s, u):
        dir_copy(0, s, u).wait_recv()
        dir_copy(1, s, u).wait_recv()
        each = STRIPS // PIECES[u]
        for p in range(PIECES[u]):
            for w in range(2):
                last_copy(w, s, u, p).wait_recv()
            for i in range(u * STRIPS + p * each, u * STRIPS + (p + 1) * each):
                span = slice(i * strip, (i + 1) * strip)
                for w in range(2):
                    whole = slice((2 * i + w) * strip, (2 * i + w + 1) * strip)
                    total = resid[s, whole].astype(F32) + part[0, s, w, span] + dir_in[1 - w, s, span] + last_in[w, s, span]
                    y_buf[s, whole] = total.astype(BF16)
            y_copy(s, u, p).start()

    factor = head_dim ** -0.5 * math.log2(math.e)
    causal = lax.broadcasted_iota(jnp.int32, (BLOCK, 2 * BLOCK), 0) <= lax.broadcasted_iota(jnp.int32, (BLOCK, 2 * BLOCK), 1) % BLOCK
    gap = jnp.zeros((head_dim, BLOCK), BF16)
    a_cols = slice(seq_len, seq_len + BLOCK)
    q_cols = slice(2 * seq_len, 2 * seq_len + BLOCK)

    def attend_block(s, u):
        for p in range(PIECES[u]):
            y_copy(s, u, p).wait_recv()
        keys = (u + 1) * BLOCK
        here = slice(u * BLOCK, (u + 1) * BLOCK)
        y = y_in[s, here].astype(F32)
        inv_rms = lax.rsqrt(jnp.mean(y * y, axis=-1, keepdims=True) + NORM_EPS)
        x = (y * inv_rms * scale[...]).astype(BF16)
        for i, (plane, cols) in enumerate(((0, q_cols), (0, here), (1, here))):
            for j in range(local):
                heads = lax.dot_general(sib_rows[i, j, 0:quarter], x, NT, preferred_element_type=F32)
                own_rows[plane, j, 0:quarter, cols] = heads.astype(BF16)

        def heads_of(step, carry):
            places = []
            for i in range(PAIRS):
                first = i % (heads_step // 2) * 2 * head_dim
                places.append((step * (PAIRS * 2 // heads_step) + i // (heads_step // 2), first))
            scores = []
            for j, first in places:
                q_one = own_rows[0, j, first:first + head_dim, q_cols]
                q_two = own_rows[0, j, first + head_dim:first + 2 * head_dim, q_cols]
                both = jnp.concatenate([jnp.concatenate([q_one, gap], axis=1), jnp.concatenate([gap, q_two], axis=1)], axis=0)
                k_pair = own_rows[0, j, first:first + 2 * head_dim, 0:keys]
                scores.append(lax.dot_general(k_pair, both, TN, preferred_element_type=F32))
            probs, sums = [], []
            for t in scores:
                diag = jnp.where(causal, t[keys - BLOCK:], -1e30)
                t = diag if u == 0 else jnp.concatenate([t[:keys - BLOCK], diag], axis=0)
                t = jnp.exp2((t - jnp.max(t, axis=0, keepdims=True)) * factor)
                sums.append(jnp.sum(t, axis=0, keepdims=True))
                probs.append(t.astype(BF16))
            for (j, first), t, total in zip(places, probs, sums):
                mixed = jnp.dot(own_rows[1, j, first:first + 2 * head_dim, 0:keys], t, preferred_element_type=F32)
                for h in range(2):
                    rows, cols = slice(h * head_dim, (h + 1) * head_dim), slice(h * BLOCK, (h + 1) * BLOCK)
                    own_rows[1, j, first + rows.start:first + rows.stop, a_cols] = (mixed[rows, cols] / total[:, cols]).astype(BF16)
            return carry

        lax.fori_loop(0, width // head_dim // (2 * PAIRS), heads_of, 0)
        proj = lax.dot_general(own_rows[1, 0, 0:quarter, a_cols], sib_rows[3, 0, 0:quarter], TN, preferred_element_type=F32)
        for j in range(1, local):
            proj += lax.dot_general(own_rows[1, j, 0:quarter, a_cols], sib_rows[3, j, 0:quarter], TN, preferred_element_type=F32)
        z = y_in[s, here].astype(F32) + proj.astype(BF16).astype(F32)
        out_ref[s, here] = z.astype(BF16)

    def final_step(s, carry):
        @pl.when(s == seqs - 2)
        def _():
            relay(seqs - 1, True)

        for u in range(blocks):
            merge_block(s, u)
            if u < blocks - 1:
                @pl.when(s == seqs - 1)
                def _():
                    attend_block(s, u)

        @pl.when(s < seqs - 1)
        def _():
            for u in range(blocks - 1):
                attend_block(s, u)

        attend_block(s, blocks - 1)
        return carry

    lax.fori_loop(0, seqs, final_step, 0)

    def drain(s, carry):
        for way in range(2):
            hop_copy(way, s).wait_send()
            for u in range(blocks):
                dir_copy(way, s, u).wait_send()
                for p in range(PIECES[u]):
                    last_copy(way, s, u, p).wait_send()
        for u in range(blocks):
            for p in range(PIECES[u]):
                y_copy(s, u, p).wait_send()
        return carry

    for rel in (2, 1, 3):
        for s in range(seqs):
            for i in range(2):
                meta_copy(rel, s, i).wait_send()
    for k in range(chips):
        for e in range(local):
            sib_copy(order(k), e).wait_send()
    lax.fori_loop(0, seqs, drain, 0)


def solution(mesh):
    ep_size, pp_size = mesh.shape['ep'], mesh.shape['pp']
    chips = ep_size // CORES
    token_spec = P(('data', 'pp'), 'ep', None, None)
    weight_spec = P('pp', None, None, None)

    def body(expert_out, expert_ids, slot_ids, gate_vals, residual, norm_scale, w_query, w_key, w_value, w_out):
        local, capacity, width = expert_out.shape[1:]
        cap = capacity // ep_size
        seqs, seq_len, tops = expert_ids.shape[1:]
        half, blocks, pieces = seq_len // 2, seq_len // BLOCK, sum(PIECES)
        assert len(PIECES) == blocks and cap // 2 < -NONE
        heads, head_dim = w_query.shape[2:]
        routing = [jnp.swapaxes(a[0], 1, 2) for a in (expert_ids, slot_ids, gate_vals)]

        def flat_t(w):
            return jnp.transpose(w[0], (1, 2, 0)).reshape(heads * head_dim, width)

        dims = (chips, pp_size, seqs, seq_len, cap, local, head_dim)
        dma = pltpu.SemaphoreType.DMA
        any_spec = pl.BlockSpec(memory_space=pl.ANY)
        vmem_spec = pl.BlockSpec(memory_space=pltpu.VMEM)
        result = pl.pallas_call(
            functools.partial(stage_kernel, dims),
            out_shape=pltpu.VMEM((seqs, seq_len, width), BF16),
            in_specs=[any_spec] * 5 + [vmem_spec] + [any_spec] * 4,
            out_specs=vmem_spec,
            scratch_shapes=[
                pltpu.VMEM((seqs, tops, seq_len), jnp.int32),
                pltpu.VMEM((seqs, tops, seq_len), jnp.int32),
                pltpu.VMEM((seqs, tops, seq_len), F32),
                pltpu.VMEM((chips, seqs, CORES * local, seq_len), BF16),
                pltpu.VMEM((chips, seqs, CORES * local, seq_len), F32),
                pltpu.VMEM((chips, seqs, CORES * local, seq_len), BF16),
                pltpu.VMEM((chips, seqs, CORES * local, seq_len), F32),
                pltpu.VMEM((2, local, cap, width), BF16),
                pltpu.VMEM((chips, local, cap, width), BF16),
                pltpu.VMEM((chips, seqs, 2, half, width), F32),
                pltpu.VMEM((2, seqs, half, width), F32),
                pltpu.VMEM((2, seqs, half, width), F32),
                pltpu.VMEM((2, seqs, half, width), F32),
                pltpu.VMEM((seqs, seq_len, width), BF16),
                pltpu.VMEM((seqs, seq_len, width), BF16),
                pltpu.VMEM((seqs, seq_len, width), BF16),
                dma((3,)), dma((2, chips, seqs)), dma((2, chips, seqs)), dma((chips, local)), dma((chips, local)), dma((2,)), dma, dma((4, local)),
                dma((2, seqs)), dma((2, seqs)), dma((2, seqs, blocks)), dma((2, seqs, blocks)),
                dma((2, seqs, pieces)), dma((2, seqs, pieces)), dma((seqs, pieces)), dma((seqs, pieces)),
            ],
            compiler_params=pltpu.CompilerParams(collective_id=0, has_side_effects=True, vmem_limit_bytes=64200000),
            name='stage',
        )(*routing, expert_out[0], residual[0], norm_scale, flat_t(w_query), flat_t(w_key), flat_t(w_value),
          w_out[0].reshape(heads * head_dim, width))
        return result[None]

    return jax.shard_map(body, mesh=mesh, in_specs=(token_spec, token_spec, token_spec, token_spec, token_spec, P('pp', None), weight_spec, weight_spec, weight_spec, weight_spec), out_specs=token_spec, check_vma=False)
```

time: 189 us -> 180 us (0.952)
  Pallas kernels: 186 us -> 179 us
    pallas_call x1, Pallas kernels: 186 us -> 179 us  [body(): pl.pallas_call(functools.partial(stage_kernel, dims), out_shape=pltpu.VME...]
where the time goes in v3:
time: 180 us
  Pallas kernels  179 us (99%)
    pallas_call x1, Pallas kernels, body(): pl.pallas_call(functools.partial(stage_kernel, dims), out_shape=pltpu.VME...  179 us

profile of v3, /device:TPU:98, one launch (start us, length us, event | category | flops | bytes accessed | tf_op | source)
XLA Modules:
  0.0 180.4 jit_solution(10727141069206763837)
XLA Ops:
  0.0 179.0 %stage.1 = bf16[3,384,1024]{2,1,0:T(8,128)(2,1)S(1)} custom-call(s32[3,8,384]{2,1,0:T(8,128)} %bitcast.35, s32[3,8,384]{2,1,0:T(8,128)} %bitcast.36, f32[3,8,384]{2,1,0:T(8,128)} %bitcast.37, bf16[4,2880,1024]{2,1,0:T(8,128)(2,1)} %bitcast.29, bf16[3,384,1024]{2,1,0:T(8,128)(2,1)} %bitcast.30, f32[1,1024]{1,0:T(1,128)} %scale.1, ...), custom_call_target="tpu_custom_call" | custom-call | tf_op jit(solution)/shard_map/stage/pallas_call | solution.py:369
  179.0 1.4 copy.12

commit v4 on v3

--- a/solution.py
+++ b/solution.py
@@ -14,7 +14,7 @@
 BLOCK = 128
 PIECES = (1, 2, 4)
 STRIPS = 4
-PAIRS = 4
+PAIRS = 8
 F32 = jnp.float32
 BF16 = jnp.bfloat16
 MESH = pl.DeviceIdType.MESH
@@ -77,21 +77,27 @@
     def hop_copy(way, s):
         return ring_copy(part.at[2, s, way], hop_in.at[way, s], hop_s.at[way, s], hop_r.at[way, s], way)
 
-    def dir_copy(way, s, u):
+    def dir_copy(way, s, u, last):
         rel = 1 if way == 0 else chips - 1
-        span = pl.ds(u * sub, sub)
+        span = pl.ds(u * sub, sub) if last else pl.ds(0, half)
         return ring_copy(part.at[rel, s, 1 - way, span], dir_in.at[way, s, span], dir_s.at[way, s, u], dir_r.at[way, s, u], way)
 
-    def last_copy(way, s, u, p):
+    def last_copy(way, s, u, p, last):
         rel = 1 if way == 0 else chips - 1
-        rows, i = sub // PIECES[u], sum(PIECES[:u]) + p
+        rows, i = sub // pieces(u, last), sum(PIECES[:u]) + p
         span = pl.ds(u * sub + p * rows, rows)
         return ring_copy(part.at[rel, s, way, span], last_in.at[way, s, span], last_s.at[way, s, i], last_r.at[way, s, i], way)
 
-    def y_copy(s, u, p):
-        rows, i = BLOCK // PIECES[u], sum(PIECES[:u]) + p
+    def y_copy(s, u, p, last):
+        rows, i = BLOCK // pieces(u, last), sum(PIECES[:u]) + p
         span = pl.ds(u * BLOCK + p * rows, rows)
         return remote(y_buf.at[s, span], y_in.at[s, span], y_s.at[s, i], y_r.at[s, i], up)
+
+    def pieces(u, last):
+        return PIECES[u] if last else 1
+
+    def dir_blocks(last):
+        return blocks if last else 1
 
     def order(k):
         return (2 + 3 * (k + k // 2 - 2 * (k // 3))) % chips
@@ -179,9 +185,9 @@
         for u in range(blocks):
             for way in range(2):
                 if last:
-                    dir_copy(way, s, u).start()
-                for p in range(PIECES[u]):
-                    last_copy(way, s, u, p).start()
+                    dir_copy(way, s, u, True).start()
+                for p in range(pieces(u, last)):
+                    last_copy(way, s, u, p, last).start()
 
     def combine_step(n, carry):
         s, k = n // chips, n % chips
@@ -218,8 +224,7 @@
         for way, ready in ((0, 1), (1, chips - 1)):
             @pl.when(jnp.logical_and(rel == ready, s < seqs - 1))
             def _():
-                for u in range(blocks):
-                    dir_copy(way, s, u).start()
+                dir_copy(way, s, 0, False).start()
 
         return carry
 
@@ -233,20 +238,21 @@
         for j in range(local):
             weight_copy(i, j).wait()
 
-    def merge_block(s, u):
-        dir_copy(0, s, u).wait_recv()
-        dir_copy(1, s, u).wait_recv()
-        each = STRIPS // PIECES[u]
-        for p in range(PIECES[u]):
+    def merge_block(s, u, last):
+        if u < dir_blocks(last):
+            dir_copy(0, s, u, last).wait_recv()
+            dir_copy(1, s, u, last).wait_recv()
+        each = STRIPS // pieces(u, last)
+        for p in range(pieces(u, last)):
             for w in range(2):
-                last_copy(w, s, u, p).wait_recv()
+                last_copy(w, s, u, p, last).wait_recv()
             for i in range(u * STRIPS + p * each, u * STRIPS + (p + 1) * each):
                 span = slice(i * strip, (i + 1) * strip)
                 for w in range(2):
                     whole = slice((2 * i + w) * strip, (2 * i + w + 1) * strip)
                     total = resid[s, whole].astype(F32) + part[0, s, w, span] + dir_in[1 - w, s, span] + last_in[w, s, span]
                     y_buf[s, whole] = total.astype(BF16)
-            y_copy(s, u, p).start()
+            y_copy(s, u, p, last).start()
 
     factor = head_dim ** -0.5 * math.log2(math.e)
     causal = lax.broadcasted_iota(jnp.int32, (BLOCK, 2 * BLOCK), 0) <= lax.broadcasted_iota(jnp.int32, (BLOCK, 2 * BLOCK), 1) % BLOCK
@@ -254,9 +260,9 @@
     a_cols = slice(seq_len, seq_len + BLOCK)
     q_cols = slice(2 * seq_len, 2 * seq_len + BLOCK)
 
-    def attend_block(s, u):
-        for p in range(PIECES[u]):
-            y_copy(s, u, p).wait_recv()
+    def attend_block(s, u, last):
+        for p in range(pieces(u, last)):
+            y_copy(s, u, p, last).wait_recv()
         keys = (u + 1) * BLOCK
         here = slice(u * BLOCK, (u + 1) * BLOCK)
         y = y_in[s, here].astype(F32)
@@ -306,33 +312,27 @@
             relay(seqs - 1, True)
 
         for u in range(blocks):
-            merge_block(s, u)
-            if u < blocks - 1:
-                @pl.when(s == seqs - 1)
-                def _():
-                    attend_block(s, u)
-
-        @pl.when(s < seqs - 1)
-        def _():
-            for u in range(blocks - 1):
-                attend_block(s, u)
-
-        attend_block(s, blocks - 1)
+            merge_block(s, u, False)
+        for u in range(blocks):
+            attend_block(s, u, False)
         return carry
 
-    lax.fori_loop(0, seqs, final_step, 0)
-
-    def drain(s, carry):
+    lax.fori_loop(0, seqs - 1, final_step, 0)
+    for u in range(blocks):
+        merge_block(seqs - 1, u, True)
+        attend_block(seqs - 1, u, True)
+
+    def drain(s, last):
         for way in range(2):
             hop_copy(way, s).wait_send()
+            for u in range(dir_blocks(last)):
+                dir_copy(way, s, u, last).wait_send()
             for u in range(blocks):
-                dir_copy(way, s, u).wait_send()
-                for p in range(PIECES[u]):
-                    last_copy(way, s, u, p).wait_send()
+                for p in range(pieces(u, last)):
+                    last_copy(way, s, u, p, last).wait_send()
         for u in range(blocks):
-            for p in range(PIECES[u]):
-                y_copy(s, u, p).wait_send()
-        return carry
+            for p in range(pieces(u, last)):
+                y_copy(s, u, p, last).wait_send()
 
     for rel in (2, 1, 3):
         for s in range(seqs):
@@ -341,7 +341,8 @@
     for k in range(chips):
         for e in range(local):
             sib_copy(order(k), e).wait_send()
-    lax.fori_loop(0, seqs, drain, 0)
+    for s in range(seqs):
+        drain(s, s == seqs - 1)
 
 
 def solution(mesh):

time: 180 us -> 180 us (level)
  no operation moved by 1% of the time
where the time goes in v4:
time: 180 us
  Pallas kernels  178 us (99%)
    pallas_call x1, Pallas kernels, body(): pl.pallas_call(functools.partial(stage_kernel, dims), out_shape=pltpu.VME...  178 us

profile of v4, /device:TPU:98, one launch (start us, length us, event | category | flops | bytes accessed | tf_op | source)
XLA Modules:
  0.0 179.5 jit_solution(8769549780760611115)
XLA Ops:
  0.0 178.1 %stage.1 = bf16[3,384,1024]{2,1,0:T(8,128)(2,1)S(1)} custom-call(s32[3,8,384]{2,1,0:T(8,128)} %bitcast.35, s32[3,8,384]{2,1,0:T(8,128)} %bitcast.36, f32[3,8,384]{2,1,0:T(8,128)} %bitcast.37, bf16[4,2880,1024]{2,1,0:T(8,128)(2,1)} %bitcast.29, bf16[3,384,1024]{2,1,0:T(8,128)(2,1)} %bitcast.30, f32[1,1024]{1,0:T(1,128)} %scale.1, ...), custom_call_target="tpu_custom_call" | custom-call | tf_op jit(solution)/shard_map/stage/pallas_call | solution.py:370
  178.1 1.4 copy.12
